TPU v7x, 32 devices: a whole 2x2x4 slice. The times are simulated.
32 devices in a mesh: table: 16 (over z, y, x), row: 2 (over core).
Axes of the slice: x: 2, y: 2, z: 4, core: 2. Of those that a mesh axis runs over, the one named last changes fastest.
Arguments:
- dense_input: bfloat16 [512, 13], P(('table', 'row')), may hold values from -6 to 6
- bottom_first: bfloat16 [13, 512], replicated, may hold values from -1.75 to 1.75
- bottom_second: bfloat16 [512, 256], replicated, may hold values from -0.375 to 0.375
- bottom_third: bfloat16 [256, 128], replicated, may hold values from -0.5 to 0.5
- wide_tables: bfloat16 [131072, 256], P(('table', 'row')), may hold values from -6 to 6
- narrow_tables: bfloat16 [131072, 64], P(('table', 'row')), may hold values from -6 to 6
- wide_indices: int32 [512, 4, 8], P(('table', 'row')), may hold values from 0 to 32767
- wide_lengths: int32 [512, 4], P(('table', 'row')), may hold values from 4 to 8
- narrow_indices: int32 [512, 4, 8], P(('table', 'row')), may hold values from 0 to 32767
- narrow_lengths: int32 [512, 4], P(('table', 'row')), may hold values from 4 to 8
- wide_projection: bfloat16 [4, 256, 128], replicated, may hold values from -0.125 to 0.125
- narrow_projection: bfloat16 [4, 64, 128], replicated, may hold values from -0.25 to 0.25
- top_first: bfloat16 [164, 1024], replicated, may hold values from -0.078125 to 0.078125
- top_last: bfloat16 [1024], replicated, may hold values from -0.1875 to 0.1875
Outputs:
- hidden: bfloat16 [512, 1024], P(('table', 'row'))
- logits: float32 [512], P(('table', 'row'))
All inputs are finite; a program needn't handle non-finite values.
Results may differ from a plain program's by a relative error of at most 0.02.
Values may be sent and summed in bfloat16 or wider, within the bound.
A program may use at most 64 MiB of HBM per device.

v0:
```python
import functools

import jax
import jax.numpy as jnp
from jax import lax
from jax.experimental import pallas as pl
from jax.experimental.pallas import tpu as pltpu
from jax.sharding import PartitionSpec as P

LOW = 256
CHUNK = 16
MESH = pl.DeviceIdType.MESH
F32 = jnp.float32
BF16 = jnp.bfloat16


def dense(values, weight):
    return jnp.maximum(jnp.dot(values, weight, preferred_element_type=F32), 0.0).astype(BF16)


def kernel(
    dims,
    x_ref,
    bf_ref,
    bs_hbm,
    bt_hbm,
    wt_hbm,
    nt_hbm,
    wi_ref,
    wl_ref,
    ni_ref,
    nl_ref,
    wp_hbm,
    np_hbm,
    tf_hbm,
    hid_ref,
    bs,
    bt,
    wt,
    nt,
    wp,
    npj,
    tf,
    send_ids,
    recv_ids,
    counts,
    give,
    got,
    part,
    recv_part,
    feats,
    local_sem,
    id_send,
    id_recv,
    part_send,
    part_recv,
    pair_send,
    pair_recv,
):
    n_table, n_row, span, tables, batch, slots, emb, rows = dims
    n = n_table * n_row
    lanes = batch * slots
    n_chunk = n // CHUNK
    owners = span * n_row
    my_table, my_row = lax.axis_index("table"), lax.axis_index("row")
    me = my_table * n_row + my_row
    own = my_table // span
    first_row = (lax.rem(my_table, span) * n_row + my_row) * rows

    def place(dev):
        return (dev // n_row, lax.rem(dev, n_row))

    def far_first(k, at, count):
        base = jnp.where(at < count // 2, count - 2 - k, k)
        return base + (base >= at).astype(jnp.int32)

    barrier = pltpu.get_barrier_semaphore()

    def greet(k, _):
        pl.semaphore_signal(
            barrier, inc=1, device_id=place(far_first(k, me, n)), device_id_type=MESH
        )
        return 0

    lax.fori_loop(0, n - 1, greet, 0, unroll=4)

    loads = [
        pltpu.make_async_copy(src, dst, local_sem.at[pos])
        for pos, (src, dst) in enumerate(
            [
                (bs_hbm, bs),
                (bt_hbm, bt),
                (tf_hbm, tf),
                (wp_hbm.at[own], wp),
                (np_hbm.at[own], npj),
                (wt_hbm, wt),
                (nt_hbm, nt),
            ]
        )
    ]
    for load in loads:
        load.start()

    past = span * n_row * rows // LOW
    slot_at = lax.broadcasted_iota(jnp.int32, (slots, batch), 0)
    spread = (
        lax.rem(lax.broadcasted_iota(jnp.int32, (batch, lanes), 1), batch)
        == lax.broadcasted_iota(jnp.int32, (batch, lanes), 0)
    ).astype(F32).astype(BF16)
    diagonal = (
        lax.broadcasted_iota(jnp.int32, (slots, lanes), 1) // batch
        == lax.broadcasted_iota(jnp.int32, (slots, lanes), 0)
    )
    for t in range(tables):
        for kind, (i_ref, l_ref) in enumerate([(wi_ref, wl_ref), (ni_ref, nl_ref)]):
            ids = i_ref[t]
            high = jnp.where(slot_at < l_ref[t : t + 1, :], ids >> (LOW.bit_length() - 1), past)
            low = ids & (LOW - 1)
            high = jnp.dot(high.astype(F32).astype(BF16), spread, preferred_element_type=F32)
            low = jnp.dot(low.astype(F32).astype(BF16), spread, preferred_element_type=F32)
            row = jnp.sum(jnp.where(diagonal, high * LOW + low, 0.0), axis=0, keepdims=True)
            send_ids[t, kind : kind + 1, :] = row.astype(jnp.int32)

    pl.semaphore_wait(barrier, n - 1)

    def send_one(k, _):
        peer = far_first(k, me, n)
        pltpu.make_async_remote_copy(
            src_ref=send_ids.at[peer // n_row // span],
            dst_ref=recv_ids.at[me],
            send_sem=id_send,
            recv_sem=id_recv,
            device_id=place(peer),
            device_id_type=MESH,
        ).start()
        return 0

    lax.fori_loop(0, n - 1, send_one, 0, unroll=4)
    pltpu.make_async_copy(send_ids.at[own], recv_ids.at[me], id_recv).start()

    bottom = dense(x_ref[...], bf_ref[...])
    loads[0].wait()
    bottom = dense(bottom, bs[...])
    loads[1].wait()
    bottom = dense(bottom, bt[...])
    feats[0] = bottom.astype(F32)
    loads[2].wait()
    base = jnp.dot(bottom, tf[0:emb, :], preferred_element_type=F32)
    for load in loads[3:]:
        load.wait()

    high_rows = rows // LOW * batch
    assert high_rows <= 256
    at_high = lax.broadcasted_iota(jnp.int32, (high_rows, lanes), 0).astype(F32).astype(BF16)
    at_low = lax.broadcasted_iota(jnp.int32, (LOW, lanes), 0).astype(F32).astype(BF16)
    one, zero = jnp.ones((), BF16), jnp.zeros((), BF16)
    sample = lax.rem(lax.broadcasted_iota(jnp.int32, (1, lanes), 1), batch)

    pltpu.make_async_copy(recv_ids, recv_ids, id_recv).wait()

    def pooled(c):
        def one_group(k, _):
            ids = recv_ids[k * n_chunk + c] - first_row
            for kind in range(2):
                local = ids[kind : kind + 1, :]
                key = (local >> (LOW.bit_length() - 1)) * batch + sample
                key = jnp.where((key >= 0) & (key < high_rows), key, -1)
                key = key.astype(F32).astype(BF16)
                digit = (local & (LOW - 1)).astype(F32).astype(BF16)
                high = jnp.where(key == at_high, one, zero)
                low = jnp.where(digit == at_low, one, zero)
                found = lax.dot_general(
                    high, low, (((1,), (1,)), ((), ())), preferred_element_type=F32
                ).astype(BF16)
                at = pl.ds(pl.multiple_of(k * batch, batch), batch)
                for h in range(rows // LOW):
                    counts[kind, at, h * LOW : (h + 1) * LOW] = found[h * batch : (h + 1) * batch]
            return 0

        lax.fori_loop(0, CHUNK, one_group, 0, unroll=4)
        wide = jnp.dot(counts[0], wt[...], preferred_element_type=F32).astype(BF16)
        wide = jnp.dot(wide, wp[...], preferred_element_type=F32)
        narrow = lax.dot_general(
            counts[1], nt[...], (((1,), (1,)), ((), ())), preferred_element_type=F32
        ).astype(BF16)
        narrow = jnp.dot(narrow, npj[...], preferred_element_type=F32)
        return wide.reshape(CHUNK, batch, emb), narrow.reshape(CHUNK, batch, emb)

    def pair_copy(c):
        return pltpu.make_async_remote_copy(
            src_ref=give.at[c],
            dst_ref=got.at[c],
            send_sem=pair_send.at[c],
            recv_sem=pair_recv.at[c],
            device_id=(my_table, 1 - my_row),
            device_id_type=MESH,
        )

    @pl.loop(0, n_chunk // n_row)
    def _(c):
        wide, narrow = pooled(c * n_row + 1 - my_row)
        give[c, :, :, 0:emb] = wide.astype(BF16)
        give[c, :, :, emb : 2 * emb] = narrow.astype(BF16)
        pair_copy(c).start()

    my_k = me // n_chunk

    @pl.loop(0, n_chunk // n_row)
    def _(c):
        wide, narrow = pooled(c * n_row + my_row)
        pair_copy(c).wait()
        part[c, :, :, 0:emb] = (wide + got[c, :, :, 0:emb].astype(F32)).astype(BF16)
        part[c, :, :, emb : 2 * emb] = (narrow + got[c, :, :, emb : 2 * emb].astype(F32)).astype(BF16)

        @pl.loop(0, CHUNK)
        def _(k):
            far = jnp.where(my_k < CHUNK // 2, CHUNK // 4 - 1 - k // 4, k // 4)
            k = far * 4 + lax.rem(my_k + k, 4)
            peer = k * n_chunk + c * n_row + my_row

            @pl.when(peer != me)
            def _():
                pltpu.make_async_remote_copy(
                    src_ref=part.at[c, k],
                    dst_ref=recv_part.at[my_table],
                    send_sem=part_send,
                    recv_sem=part_recv,
                    device_id=place(peer),
                    device_id_type=MESH,
                ).start()

            @pl.when(peer == me)
            def _():
                pltpu.make_async_copy(part.at[c, k], recv_part.at[my_table], part_recv).start()

    pltpu.make_async_copy(recv_part, recv_part, part_recv).wait()

    for t in range(tables):
        total = recv_part[t * span].astype(F32)
        for s in range(1, span):
            total = total + recv_part[t * span + s].astype(F32)
        total = total.astype(BF16).astype(F32)
        feats[1 + t] = total[:, 0:emb]
        feats[1 + tables + t] = total[:, emb : 2 * emb]

    features = 1 + 2 * tables
    pairs = features * (features - 1) // 2
    column = lax.broadcasted_iota(jnp.int32, (batch, pairs), 1)
    values = jnp.zeros((batch, pairs), F32)
    if features <= 16:
        held = [feats[f] for f in range(features)]
        pos = 0
        for f in range(features):
            for g in range(f + 1, features):
                value = jnp.sum(held[f] * held[g], axis=1, keepdims=True)
                values = jnp.where(column == pos, value, values)
                pos += 1
    else:

        def outer(f, values):
            mine = feats[f]
            start = f * features - f * (f + 1) // 2 - f - 1

            def inner(g, values):
                value = jnp.sum(mine * feats[g], axis=1, keepdims=True)
                return jnp.where(column == start + g, value, values)

            return lax.fori_loop(f + 1, features, inner, values)

        values = lax.fori_loop(0, features - 1, outer, values)
    hidden = base + jnp.dot(
        values.astype(BF16), tf[emb : emb + pairs, :], preferred_element_type=F32
    )
    hidden = jnp.maximum(hidden, 0.0).astype(BF16)
    hid_ref[...] = hidden

    pltpu.make_async_copy(
        recv_ids.at[pl.ds(0, n - 1)], recv_ids.at[pl.ds(0, n - 1)], id_send
    ).wait()
    pltpu.make_async_copy(
        recv_part.at[pl.ds(0, n_table - 1)], recv_part.at[pl.ds(0, n_table - 1)], part_send
    ).wait()


def last_kernel(hid_ref, tl_ref, out_ref, log_ref):
    out_ref[...] = hid_ref[...]
    total = jnp.zeros(log_ref.shape, F32)
    size = tl_ref.shape[1]
    for j in range(tl_ref.shape[0]):
        total = total + lax.dot_general(
            tl_ref[j : j + 1, :],
            hid_ref[:, j * size : (j + 1) * size],
            (((1,), (1,)), ((), ())),
            preferred_element_type=F32,
        )
    log_ref[...] = total


def body(
    dense_input,
    bottom_first,
    bottom_second,
    bottom_third,
    wide_tables,
    narrow_tables,
    wide_indices,
    wide_lengths,
    narrow_indices,
    narrow_lengths,
    wide_projection,
    narrow_projection,
    top_first,
    top_last,
):
    n_table, n_row = lax.axis_size("table"), lax.axis_size("row")
    tables = wide_projection.shape[0]
    span = n_table // tables
    n = n_table * n_row
    batch, slots = dense_input.shape[0], wide_indices.shape[2]
    emb = wide_projection.shape[2]
    rows, width = wide_tables.shape
    top = top_first.shape[1]
    dims = (n_table, n_row, span, tables, batch, slots, emb, rows)
    n_chunk = n // CHUNK
    vmem = pl.BlockSpec(memory_space=pltpu.VMEM)
    hbm = pl.BlockSpec(memory_space=pl.ANY)

    def like(a):
        return pltpu.VMEM(a.shape, a.dtype)

    hidden = pl.pallas_call(
        functools.partial(kernel, dims),
        out_shape=jax.ShapeDtypeStruct((batch, top), BF16),
        in_specs=[vmem, vmem, hbm, hbm, hbm, hbm, vmem, vmem, vmem, vmem, hbm, hbm, hbm],
        out_specs=vmem,
        scratch_shapes=[
            like(bottom_second),
            like(bottom_third),
            like(wide_tables),
            pltpu.VMEM(narrow_tables.shape[::-1], BF16),
            pltpu.VMEM(wide_projection.shape[1:], BF16),
            pltpu.VMEM(narrow_projection.shape[1:], BF16),
            like(top_first),
            pltpu.VMEM((tables, 2, batch * slots), jnp.int32),
            pltpu.VMEM((n, 2, batch * slots), jnp.int32),
            pltpu.VMEM((2, CHUNK * batch, rows), BF16),
            pltpu.VMEM((n_chunk // n_row, CHUNK, batch, 2 * emb), BF16),
            pltpu.VMEM((n_chunk // n_row, CHUNK, batch, 2 * emb), BF16),
            pltpu.VMEM((n_chunk // n_row, CHUNK, batch, 2 * emb), BF16),
            pltpu.VMEM((n_table, batch, 2 * emb), BF16),
            pltpu.VMEM((1 + 2 * tables, batch, emb), F32),
            pltpu.SemaphoreType.DMA((7,)),
            pltpu.SemaphoreType.DMA,
            pltpu.SemaphoreType.DMA,
            pltpu.SemaphoreType.DMA,
            pltpu.SemaphoreType.DMA,
            pltpu.SemaphoreType.DMA((n_chunk // n_row,)),
            pltpu.SemaphoreType.DMA((n_chunk // n_row,)),
        ],
        compiler_params=pltpu.CompilerParams(
            collective_id=0, has_side_effects=True, vmem_limit_bytes=60 * 2**20
        ),
    )(
        dense_input,
        bottom_first,
        bottom_second,
        bottom_third,
        wide_tables,
        narrow_tables.T,
        wide_indices.transpose(1, 2, 0),
        wide_lengths.T,
        narrow_indices.transpose(1, 2, 0),
        narrow_lengths.T,
        wide_projection,
        narrow_projection,
        top_first,
    )
    hidden, logits = pl.pallas_call(
        last_kernel,
        out_shape=(
            jax.ShapeDtypeStruct((batch, top), BF16),
            jax.ShapeDtypeStruct((1, batch), F32),
        ),
        in_specs=[vmem, vmem],
        out_specs=(vmem, vmem),
    )(hidden, top_last.reshape(-1, emb))
    return hidden, logits.reshape(-1)


def solution(mesh):
    split = ("table", "row")
    in_specs = (
        P(split, None),
        P(),
        P(),
        P(),
        P(split, None),
        P(split, None),
        P(split, None, None),
        P(split, None),
        P(split, None, None),
        P(split, None),
        P(),
        P(),
        P(),
        P(),
    )
    out_specs = (P(split, None), P(split))
    return jax.shard_map(body, mesh=mesh, in_specs=in_specs, out_specs=out_specs, check_vma=False)
```

profile of v0, /device:TPU:0, one launch (start us, length us, event | category | flops | bytes accessed | tf_op | source)
XLA Modules:
  0.0 28.6 jit_solution(4321779280824492244)
XLA Ops:
  0.6 26.6 %shard_map.149.hid_ref = bf16[16,1024]{1,0:T(8,128)(2,1)} custom-call(bf16[16,13]{1,0:T(8,128)(2,1)} %x_ref.1, bf16[13,512]{1,0:T(8,128)(2,1)} %bf_ref.1, bf16[512,256]{1,0:T(8,128)(2,1)} %bs_hbm.1, bf16[256,128]{1,0:T(8,128)(2,1)} %bt_hbm.1, bf16[4096,256]{1,0:T(8,128)(2,1)} %wt_hbm.1, bf16[64,4096]{1,0:T(8,128)(2,1)} %bitcast.7, s32[4,8,16]{2,1,0:T(8,128)} %bitcast.8, ...), custom_call_target="tpu_custom_call" | custom-call | tf_op jit(solution)/shard_map/pallas_call | solution.py:331
  27.2 1.4 %shard_map.150 = (bf16[16,1024]{1,0:T(8,128)(2,1)}, f32[1,16]{1,0:T(1,128)}) custom-call(bf16[16,1024]{1,0:T(8,128)(2,1)} %shard_map.149.hid_ref, bf16[8,128]{1,0:T(8,128)(2,1)} %bitcast.12), custom_call_target="tpu_custom_call" | custom-call | tf_op jit(solution)/shard_map/pallas_call | solution.py:378
where the time goes:
time: 28.9 us; the launch traced here: 28.6 us
  Pallas kernels  28 us (97%)
  between operations  0.64 us (2%)
    pallas_call x1, Pallas kernels, body(): pl.pallas_call(functools.partial(kernel, dims), out_shape=jax.ShapeDtypeS...  26.6 us
    pallas_call x1, Pallas kernels, body(): pl.pallas_call(last_kernel, out_shape=(jax.ShapeDtypeStruct((batch, top),...  1.42 us

commit v1 on v0

--- a/solution.py
+++ b/solution.py
@@ -8,6 +8,8 @@
 from jax.sharding import PartitionSpec as P
 
 LOW = 256
+PROJECT = 512
+BASE = 32
 CHUNK = 16
 MESH = pl.DeviceIdType.MESH
 F32 = jnp.float32
@@ -20,20 +22,26 @@
 
 def kernel(
     dims,
-    x_ref,
-    bf_ref,
+    x_hbm,
+    bf_hbm,
     bs_hbm,
     bt_hbm,
     wt_hbm,
     nt_hbm,
+    wi_hbm,
+    wl_hbm,
+    ni_hbm,
+    nl_hbm,
+    wp_hbm,
+    np_hbm,
+    tf_hbm,
+    hid_ref,
+    x_ref,
+    bf_ref,
     wi_ref,
     wl_ref,
     ni_ref,
     nl_ref,
-    wp_hbm,
-    np_hbm,
-    tf_hbm,
-    hid_ref,
     bs,
     bt,
     wt,
@@ -44,6 +52,8 @@
     send_ids,
     recv_ids,
     counts,
+    flat_wide,
+    flat_narrow,
     give,
     got,
     part,
@@ -88,6 +98,12 @@
         pltpu.make_async_copy(src, dst, local_sem.at[pos])
         for pos, (src, dst) in enumerate(
             [
+                (wi_hbm, wi_ref),
+                (wl_hbm, wl_ref),
+                (ni_hbm, ni_ref),
+                (nl_hbm, nl_ref),
+                (x_hbm, x_ref),
+                (bf_hbm, bf_ref),
                 (bs_hbm, bs),
                 (bt_hbm, bt),
                 (tf_hbm, tf),
@@ -101,6 +117,8 @@
     for load in loads:
         load.start()
 
+    for load in loads[:4]:
+        load.wait()
     past = span * n_row * rows // LOW
     slot_at = lax.broadcasted_iota(jnp.int32, (slots, batch), 0)
     spread = (
@@ -138,52 +156,70 @@
     lax.fori_loop(0, n - 1, send_one, 0, unroll=4)
     pltpu.make_async_copy(send_ids.at[own], recv_ids.at[me], id_recv).start()
 
+    for load in loads[4:6]:
+        load.wait()
     bottom = dense(x_ref[...], bf_ref[...])
-    loads[0].wait()
+    loads[6].wait()
     bottom = dense(bottom, bs[...])
-    loads[1].wait()
+    loads[7].wait()
     bottom = dense(bottom, bt[...])
     feats[0] = bottom.astype(F32)
-    loads[2].wait()
+    loads[8].wait()
     base = jnp.dot(bottom, tf[0:emb, :], preferred_element_type=F32)
-    for load in loads[3:]:
+    for load in loads[9:]:
         load.wait()
 
-    high_rows = rows // LOW * batch
+    high_count = rows // LOW
+    high_rows = high_count * batch
     assert high_rows <= 256
+    for r in range(0, rows, PROJECT):
+        at = pl.ds(r, PROJECT)
+        flat_wide[at, :] = jnp.dot(
+            wt[at, :], wp[...], preferred_element_type=F32
+        ).astype(BF16)
+        flat_narrow[at, :] = lax.dot_general(
+            nt[:, at], npj[...], (((0,), (0,)), ((), ())), preferred_element_type=F32
+        ).astype(BF16)
+
     at_high = lax.broadcasted_iota(jnp.int32, (high_rows, lanes), 0).astype(F32).astype(BF16)
     at_low = lax.broadcasted_iota(jnp.int32, (LOW, lanes), 0).astype(F32).astype(BF16)
     one, zero = jnp.ones((), BF16), jnp.zeros((), BF16)
+    marks = [one, jnp.full((), -BASE, BF16)]
+    shift = jnp.full((), 192 * BASE, BF16)
     sample = lax.rem(lax.broadcasted_iota(jnp.int32, (1, lanes), 1), batch)
 
     pltpu.make_async_copy(recv_ids, recv_ids, id_recv).wait()
 
     def pooled(c):
-        def one_group(k, _):
+        for k in range(CHUNK):
             ids = recv_ids[k * n_chunk + c] - first_row
+            high, low = [], []
             for kind in range(2):
                 local = ids[kind : kind + 1, :]
                 key = (local >> (LOW.bit_length() - 1)) * batch + sample
                 key = jnp.where((key >= 0) & (key < high_rows), key, -1)
                 key = key.astype(F32).astype(BF16)
                 digit = (local & (LOW - 1)).astype(F32).astype(BF16)
-                high = jnp.where(key == at_high, one, zero)
-                low = jnp.where(digit == at_low, one, zero)
-                found = lax.dot_general(
-                    high, low, (((1,), (1,)), ((), ())), preferred_element_type=F32
-                ).astype(BF16)
-                at = pl.ds(pl.multiple_of(k * batch, batch), batch)
-                for h in range(rows // LOW):
-                    counts[kind, at, h * LOW : (h + 1) * LOW] = found[h * batch : (h + 1) * batch]
-            return 0
-
-        lax.fori_loop(0, CHUNK, one_group, 0, unroll=4)
-        wide = jnp.dot(counts[0], wt[...], preferred_element_type=F32).astype(BF16)
-        wide = jnp.dot(wide, wp[...], preferred_element_type=F32)
-        narrow = lax.dot_general(
-            counts[1], nt[...], (((1,), (1,)), ((), ())), preferred_element_type=F32
-        ).astype(BF16)
-        narrow = jnp.dot(narrow, npj[...], preferred_element_type=F32)
+                high.append(jnp.where(key == at_high, marks[kind], zero))
+                low.append(jnp.where(digit == at_low, one, zero))
+            found = lax.dot_general(
+                jnp.concatenate(high, axis=1),
+                jnp.concatenate(low, axis=1),
+                (((1,), (1,)), ((), ())),
+                preferred_element_type=F32,
+            ).astype(BF16)
+            for h in range(high_count):
+                counts[h, k * batch : (k + 1) * batch, :] = found[h * batch : (h + 1) * batch]
+        wide = jnp.zeros((CHUNK * batch, emb), F32)
+        narrow = jnp.zeros((CHUNK * batch, emb), F32)
+        for h in range(high_count):
+            both = counts[h]
+            second = (both + shift) - shift
+            first = both - second
+            at = slice(h * LOW, (h + 1) * LOW)
+            wide = wide + jnp.dot(first, flat_wide[at, :], preferred_element_type=F32)
+            narrow = narrow + jnp.dot(second, flat_narrow[at, :], preferred_element_type=F32)
+        narrow = narrow * (-1.0 / BASE)
         return wide.reshape(CHUNK, batch, emb), narrow.reshape(CHUNK, batch, emb)
 
     def pair_copy(c):
@@ -330,10 +366,16 @@
 
     hidden = pl.pallas_call(
         functools.partial(kernel, dims),
-        out_shape=jax.ShapeDtypeStruct((batch, top), BF16),
-        in_specs=[vmem, vmem, hbm, hbm, hbm, hbm, vmem, vmem, vmem, vmem, hbm, hbm, hbm],
+        out_shape=pltpu.VMEM((batch, top), BF16),
+        in_specs=[hbm] * 13,
         out_specs=vmem,
         scratch_shapes=[
+            like(dense_input),
+            like(bottom_first),
+            pltpu.VMEM((tables, slots, batch), jnp.int32),
+            pltpu.VMEM((tables, batch), jnp.int32),
+            pltpu.VMEM((tables, slots, batch), jnp.int32),
+            pltpu.VMEM((tables, batch), jnp.int32),
             like(bottom_second),
             like(bottom_third),
             like(wide_tables),
@@ -343,13 +385,15 @@
             like(top_first),
             pltpu.VMEM((tables, 2, batch * slots), jnp.int32),
             pltpu.VMEM((n, 2, batch * slots), jnp.int32),
-            pltpu.VMEM((2, CHUNK * batch, rows), BF16),
+            pltpu.VMEM((rows // LOW, CHUNK * batch, LOW), BF16),
+            pltpu.VMEM((rows, emb), BF16),
+            pltpu.VMEM((rows, emb), BF16),
             pltpu.VMEM((n_chunk // n_row, CHUNK, batch, 2 * emb), BF16),
             pltpu.VMEM((n_chunk // n_row, CHUNK, batch, 2 * emb), BF16),
             pltpu.VMEM((n_chunk // n_row, CHUNK, batch, 2 * emb), BF16),
             pltpu.VMEM((n_table, batch, 2 * emb), BF16),
             pltpu.VMEM((1 + 2 * tables, batch, emb), F32),
-            pltpu.SemaphoreType.DMA((7,)),
+            pltpu.SemaphoreType.DMA((13,)),
             pltpu.SemaphoreType.DMA,
             pltpu.SemaphoreType.DMA,
             pltpu.SemaphoreType.DMA,
@@ -358,7 +402,7 @@
             pltpu.SemaphoreType.DMA((n_chunk // n_row,)),
         ],
         compiler_params=pltpu.CompilerParams(
-            collective_id=0, has_side_effects=True, vmem_limit_bytes=60 * 2**20
+            collective_id=0, has_side_effects=True, vmem_limit_bytes=int(60 * 2**20)
         ),
     )(
         dense_input,
@@ -383,6 +427,7 @@
         ),
         in_specs=[vmem, vmem],
         out_specs=(vmem, vmem),
+        compiler_params=pltpu.CompilerParams(vmem_limit_bytes=4 * 2**20),
     )(hidden, top_last.reshape(-1, emb))
     return hidden, logits.reshape(-1)
 

time: 28.9 us -> 21.9 us (0.76)
  Pallas kernels: 28 us -> 21.1 us
    pallas_call x1, Pallas kernels: 26.6 us -> 20.4 us  [body(): pl.pallas_call(functools.partial(kernel, dims), out_shape=pltpu.VMEM((bat...]
    pallas_call x1, Pallas kernels: 1.42 us -> 0.66 us  [body(): pl.pallas_call(last_kernel, out_shape=(jax.ShapeDtypeStruct((batch, top),...]
where the time goes in v1:
time: 21.9 us; the launch traced here: 21.8 us
  Pallas kernels  21.1 us (96%)
  between operations  0.66 us (3%)
    pallas_call x1, Pallas kernels, body(): pl.pallas_call(functools.partial(kernel, dims), out_shape=pltpu.VMEM((bat...  20.4 us
    pallas_call x1, Pallas kernels, body(): pl.pallas_call(last_kernel, out_shape=(jax.ShapeDtypeStruct((batch, top),...  0.66 us

profile of v1, /device:TPU:0, one launch (start us, length us, event | category | flops | bytes accessed | tf_op | source)
XLA Modules:
  0.0 21.8 jit_solution(17473910825362323896)
XLA Ops:
  0.6 0.0 copy-start
  0.6 20.4 %shard_map.149.hid_ref = bf16[16,1024]{1,0:T(8,128)(2,1)S(1)} custom-call(bf16[16,13]{1,0:T(8,128)(2,1)} %x_hbm.1, bf16[13,512]{1,0:T(8,128)(2,1)} %bf_hbm.1, bf16[512,256]{1,0:T(8,128)(2,1)} %bs_hbm.1, bf16[256,128]{1,0:T(8,128)(2,1)} %bt_hbm.1, bf16[4096,256]{1,0:T(8,128)(2,1)} %wt_hbm.1, bf16[64,4096]{1,0:T(8,128)(2,1)} %bitcast.8, s32[4,8,16]{2,1,0:T(8,128)} %bitcast.9, ...), custom_call_target="tpu_custom_call" | custom-call | tf_op jit(solution)/shard_map/pallas_call | solution.py:367
  21.1 0.0 copy-done
  21.1 0.7 %shard_map.150 = (bf16[16,1024]{1,0:T(8,128)(2,1)}, f32[1,16]{1,0:T(1,128)}) custom-call(bf16[16,1024]{1,0:T(8,128)(2,1)S(1)} %shard_map.149.hid_ref, bf16[8,128]{1,0:T(8,128)(2,1)S(1)} %bitcast.7), custom_call_target="tpu_custom_call" | custom-call | tf_op jit(solution)/shard_map/pallas_call | solution.py:422
Async XLA Ops:
  0.6 20.5 %copy-start = (bf16[1024]{0:T(1024)(128)(2,1)S(1)}, bf16[1024]{0:T(1024)(128)(2,1)}, u32[]{:S(2)}) copy-start(bf16[1024]{0:T(1024)(128)(2,1)} %param.27) | copy-start | bytes 6148

commit v2 on v1

--- a/solution.py
+++ b/solution.py
@@ -10,7 +10,10 @@
 LOW = 256
 PROJECT = 512
 BASE = 32
-CHUNK = 16
+SIDES = 4
+SIDE = 4
+CHUNK = SIDES * SIDE
+PLAN = ((0,0,None,None),(1,1,0,None),(2,2,1,0),(3,3,None,None),(None,None,3,1),(None,None,2,3),(None,None,None,2))
 MESH = pl.DeviceIdType.MESH
 F32 = jnp.float32
 BF16 = jnp.bfloat16
@@ -56,6 +59,7 @@
     flat_narrow,
     give,
     got,
+    keep,
     part,
     recv_part,
     feats,
@@ -71,6 +75,8 @@
     n = n_table * n_row
     lanes = batch * slots
     n_chunk = n // CHUNK
+    n_cc = n_chunk // n_row
+    n_side = n_table // SIDES
     owners = span * n_row
     my_table, my_row = lax.axis_index("table"), lax.axis_index("row")
     me = my_table * n_row + my_row
@@ -142,19 +148,19 @@
     pl.semaphore_wait(barrier, n - 1)
 
     def send_one(k, _):
-        peer = far_first(k, me, n)
+        peer = me ^ jnp.where(k < n // 2, n // 2 + k, k + 1 - n // 2)
         pltpu.make_async_remote_copy(
             src_ref=send_ids.at[peer // n_row // span],
             dst_ref=recv_ids.at[me],
             send_sem=id_send,
-            recv_sem=id_recv,
+            recv_sem=id_recv.at[my_table // n_side],
             device_id=place(peer),
             device_id_type=MESH,
         ).start()
         return 0
 
     lax.fori_loop(0, n - 1, send_one, 0, unroll=4)
-    pltpu.make_async_copy(send_ids.at[own], recv_ids.at[me], id_recv).start()
+    pltpu.make_async_copy(send_ids.at[own], recv_ids.at[me], id_recv.at[my_table // n_side]).start()
 
     for load in loads[4:6]:
         load.wait()
@@ -177,9 +183,10 @@
         flat_wide[at, :] = jnp.dot(
             wt[at, :], wp[...], preferred_element_type=F32
         ).astype(BF16)
-        flat_narrow[at, :] = lax.dot_general(
+        narrow = lax.dot_general(
             nt[:, at], npj[...], (((0,), (0,)), ((), ())), preferred_element_type=F32
-        ).astype(BF16)
+        )
+        flat_narrow[at, :] = (narrow * (-1.0 / BASE)).astype(BF16)
 
     at_high = lax.broadcasted_iota(jnp.int32, (high_rows, lanes), 0).astype(F32).astype(BF16)
     at_low = lax.broadcasted_iota(jnp.int32, (LOW, lanes), 0).astype(F32).astype(BF16)
@@ -188,86 +195,110 @@
     shift = jnp.full((), 192 * BASE, BF16)
     sample = lax.rem(lax.broadcasted_iota(jnp.int32, (1, lanes), 1), batch)
 
-    pltpu.make_async_copy(recv_ids, recv_ids, id_recv).wait()
-
-    def pooled(c):
-        for k in range(CHUNK):
-            ids = recv_ids[k * n_chunk + c] - first_row
-            high, low = [], []
-            for kind in range(2):
-                local = ids[kind : kind + 1, :]
-                key = (local >> (LOW.bit_length() - 1)) * batch + sample
-                key = jnp.where((key >= 0) & (key < high_rows), key, -1)
-                key = key.astype(F32).astype(BF16)
-                digit = (local & (LOW - 1)).astype(F32).astype(BF16)
-                high.append(jnp.where(key == at_high, marks[kind], zero))
-                low.append(jnp.where(digit == at_low, one, zero))
-            found = lax.dot_general(
-                jnp.concatenate(high, axis=1),
-                jnp.concatenate(low, axis=1),
-                (((1,), (1,)), ((), ())),
-                preferred_element_type=F32,
-            ).astype(BF16)
-            for h in range(high_count):
-                counts[h, k * batch : (k + 1) * batch, :] = found[h * batch : (h + 1) * batch]
-        wide = jnp.zeros((CHUNK * batch, emb), F32)
-        narrow = jnp.zeros((CHUNK * batch, emb), F32)
+    my_side = my_table // n_side
+
+    def side_of(step):
+        if not step:
+            return my_side
+        side = SIDES - step
+        return jnp.where(side > my_side, side, side - 1)
+
+    def each(body):
+        if n_cc == 1:
+            body(0)
+        else:
+            pl.loop(0, n_cc)(body)
+
+    def count(step, cc):
+        first_k = side_of(step) * SIDE
+        for place_row in range(n_row):
+            row = lax.rem(my_row + place_row, n_row)
+            for k in range(SIDE):
+                at = (place_row * SIDE + k) * batch
+                ids = recv_ids[(first_k + k) * n_chunk + cc * n_row + row] - first_row
+                high, low = [], []
+                for kind in range(2):
+                    local = ids[kind : kind + 1, :]
+                    key = (local >> (LOW.bit_length() - 1)) * batch + sample
+                    key = jnp.where((key >= 0) & (key < high_rows), key, -1)
+                    key = key.astype(F32).astype(BF16)
+                    digit = (local & (LOW - 1)).astype(F32).astype(BF16)
+                    high.append(jnp.where(key == at_high, marks[kind], zero))
+                    low.append(jnp.where(digit == at_low, one, zero))
+                found = lax.dot_general(
+                    jnp.concatenate(high, axis=1),
+                    jnp.concatenate(low, axis=1),
+                    (((1,), (1,)), ((), ())),
+                    preferred_element_type=F32,
+                ).astype(BF16)
+                for h in range(high_count):
+                    counts[step, cc, h, at : at + batch, :] = found[h * batch : (h + 1) * batch]
+
+    def weigh(step, cc):
+        wide = jnp.zeros((SIDE * n_row * batch, emb), F32)
+        narrow = jnp.zeros((SIDE * n_row * batch, emb), F32)
         for h in range(high_count):
-            both = counts[h]
+            both = counts[step, cc, h]
             second = (both + shift) - shift
             first = both - second
             at = slice(h * LOW, (h + 1) * LOW)
             wide = wide + jnp.dot(first, flat_wide[at, :], preferred_element_type=F32)
             narrow = narrow + jnp.dot(second, flat_narrow[at, :], preferred_element_type=F32)
-        narrow = narrow * (-1.0 / BASE)
-        return wide.reshape(CHUNK, batch, emb), narrow.reshape(CHUNK, batch, emb)
-
-    def pair_copy(c):
+        given = SIDE * batch
+        for half, value in enumerate((wide, narrow)):
+            at = slice(half * emb, (half + 1) * emb)
+            give[step, cc, :, at] = value[:given].astype(BF16)
+            keep[step, cc, :, at] = value[given:]
+        pair_copy(step, cc).start()
+
+    def pair_copy(step, cc):
         return pltpu.make_async_remote_copy(
-            src_ref=give.at[c],
-            dst_ref=got.at[c],
-            send_sem=pair_send.at[c],
-            recv_sem=pair_recv.at[c],
+            src_ref=give.at[step, cc],
+            dst_ref=got.at[step, cc],
+            send_sem=pair_send.at[step, cc],
+            recv_sem=pair_recv.at[step, cc],
             device_id=(my_table, 1 - my_row),
             device_id_type=MESH,
         )
 
-    @pl.loop(0, n_chunk // n_row)
-    def _(c):
-        wide, narrow = pooled(c * n_row + 1 - my_row)
-        give[c, :, :, 0:emb] = wide.astype(BF16)
-        give[c, :, :, emb : 2 * emb] = narrow.astype(BF16)
-        pair_copy(c).start()
-
-    my_k = me // n_chunk
-
-    @pl.loop(0, n_chunk // n_row)
-    def _(c):
-        wide, narrow = pooled(c * n_row + my_row)
-        pair_copy(c).wait()
-        part[c, :, :, 0:emb] = (wide + got[c, :, :, 0:emb].astype(F32)).astype(BF16)
-        part[c, :, :, emb : 2 * emb] = (narrow + got[c, :, :, emb : 2 * emb].astype(F32)).astype(BF16)
-
-        @pl.loop(0, CHUNK)
-        def _(k):
-            far = jnp.where(my_k < CHUNK // 2, CHUNK // 4 - 1 - k // 4, k // 4)
-            k = far * 4 + lax.rem(my_k + k, 4)
-            peer = k * n_chunk + c * n_row + my_row
-
-            @pl.when(peer != me)
-            def _():
+    def arrive(step):
+        side = side_of(step)
+        arrived = recv_ids.at[pl.ds(side * (n // SIDES), n // SIDES)]
+        pltpu.make_async_copy(arrived, arrived, id_recv.at[side]).wait()
+
+    def finish(step):
+        side = side_of(step)
+
+        def block(cc):
+            pair_copy(step, cc).wait()
+            part[step, cc] = (keep[step, cc] + got[step, cc].astype(F32)).astype(BF16)
+            for k in range(SIDE):
+                peer = (side * SIDE + k) * n_cc + cc
+
                 pltpu.make_async_remote_copy(
-                    src_ref=part.at[c, k],
+                    src_ref=part.at[step, cc, pl.ds(k * batch, batch)],
                     dst_ref=recv_part.at[my_table],
                     send_sem=part_send,
                     recv_sem=part_recv,
-                    device_id=place(peer),
+                    device_id=(peer, 1 - my_row),
                     device_id_type=MESH,
                 ).start()
 
-            @pl.when(peer == me)
-            def _():
-                pltpu.make_async_copy(part.at[c, k], recv_part.at[my_table], part_recv).start()
+        each(block)
+
+    for waits, counted, weighed, finished in PLAN:
+        if waits is not None:
+            arrive(waits)
+
+        def block(cc):
+            if counted is not None:
+                count(counted, cc)
+            if weighed is not None:
+                weigh(weighed, cc)
+
+        each(block)
+        if finished is not None:
+            finish(finished)
 
     pltpu.make_async_copy(recv_part, recv_part, part_recv).wait()
 
@@ -313,9 +344,7 @@
     pltpu.make_async_copy(
         recv_ids.at[pl.ds(0, n - 1)], recv_ids.at[pl.ds(0, n - 1)], id_send
     ).wait()
-    pltpu.make_async_copy(
-        recv_part.at[pl.ds(0, n_table - 1)], recv_part.at[pl.ds(0, n_table - 1)], part_send
-    ).wait()
+    pltpu.make_async_copy(recv_part, recv_part, part_send).wait()
 
 
 def last_kernel(hid_ref, tl_ref, out_ref, log_ref):
@@ -357,7 +386,7 @@
     rows, width = wide_tables.shape
     top = top_first.shape[1]
     dims = (n_table, n_row, span, tables, batch, slots, emb, rows)
-    n_chunk = n // CHUNK
+    n_cc = n // CHUNK // n_row
     vmem = pl.BlockSpec(memory_space=pltpu.VMEM)
     hbm = pl.BlockSpec(memory_space=pl.ANY)
 
@@ -385,21 +414,19 @@
             like(top_first),
             pltpu.VMEM((tables, 2, batch * slots), jnp.int32),
             pltpu.VMEM((n, 2, batch * slots), jnp.int32),
-            pltpu.VMEM((rows // LOW, CHUNK * batch, LOW), BF16),
+            pltpu.VMEM((SIDES, n_cc, rows // LOW, SIDE * n_row * batch, LOW), BF16),
             pltpu.VMEM((rows, emb), BF16),
             pltpu.VMEM((rows, emb), BF16),
-            pltpu.VMEM((n_chunk // n_row, CHUNK, batch, 2 * emb), BF16),
-            pltpu.VMEM((n_chunk // n_row, CHUNK, batch, 2 * emb), BF16),
-            pltpu.VMEM((n_chunk // n_row, CHUNK, batch, 2 * emb), BF16),
+            *[pltpu.VMEM((SIDES, n_cc, SIDE * batch, 2 * emb), d) for d in (BF16, BF16, F32, BF16)],
             pltpu.VMEM((n_table, batch, 2 * emb), BF16),
             pltpu.VMEM((1 + 2 * tables, batch, emb), F32),
             pltpu.SemaphoreType.DMA((13,)),
             pltpu.SemaphoreType.DMA,
+            pltpu.SemaphoreType.DMA((SIDES,)),
             pltpu.SemaphoreType.DMA,
             pltpu.SemaphoreType.DMA,
-            pltpu.SemaphoreType.DMA,
-            pltpu.SemaphoreType.DMA((n_chunk // n_row,)),
-            pltpu.SemaphoreType.DMA((n_chunk // n_row,)),
+            pltpu.SemaphoreType.DMA((SIDES, n_cc)),
+            pltpu.SemaphoreType.DMA((SIDES, n_cc)),
         ],
         compiler_params=pltpu.CompilerParams(
             collective_id=0, has_side_effects=True, vmem_limit_bytes=int(60 * 2**20)

time: 21.9 us -> 20.5 us (0.936)
  Pallas kernels: 21.1 us -> 19.6 us
    pallas_call x1, Pallas kernels: 20.4 us -> 18.9 us  [body(): pl.pallas_call(functools.partial(kernel, dims), out_shape=pltpu.VMEM((bat...]
where the time goes in v2:
time: 20.5 us; the launch traced here: 20.3 us
  Pallas kernels  19.6 us (96%)
  between operations  0.66 us (3%)
    pallas_call x1, Pallas kernels, body(): pl.pallas_call(functools.partial(kernel, dims), out_shape=pltpu.VMEM((bat...  18.9 us
    pallas_call x1, Pallas kernels, body(): pl.pallas_call(last_kernel, out_shape=(jax.ShapeDtypeStruct((batch, top),...  0.66 us

profile of v2, /device:TPU:0, one launch (start us, length us, event | category | flops | bytes accessed | tf_op | source)
XLA Modules:
  0.0 20.3 jit_solution(3565912367186413381)
XLA Ops:
  0.6 0.0 copy-start
  0.6 18.9 %shard_map.149.hid_ref = bf16[16,1024]{1,0:T(8,128)(2,1)S(1)} custom-call(bf16[16,13]{1,0:T(8,128)(2,1)} %x_hbm.1, bf16[13,512]{1,0:T(8,128)(2,1)} %bf_hbm.1, bf16[512,256]{1,0:T(8,128)(2,1)} %bs_hbm.1, bf16[256,128]{1,0:T(8,128)(2,1)} %bt_hbm.1, bf16[4096,256]{1,0:T(8,128)(2,1)} %wt_hbm.1, bf16[64,4096]{1,0:T(8,128)(2,1)} %bitcast.8, s32[4,8,16]{2,1,0:T(8,128)} %bitcast.9, ...), custom_call_target="tpu_custom_call" | custom-call | tf_op jit(solution)/shard_map/pallas_call | solution.py:396
  19.6 0.0 copy-done
  19.6 0.7 %shard_map.150 = (bf16[16,1024]{1,0:T(8,128)(2,1)}, f32[1,16]{1,0:T(1,128)}) custom-call(bf16[16,1024]{1,0:T(8,128)(2,1)S(1)} %shard_map.149.hid_ref, bf16[8,128]{1,0:T(8,128)(2,1)S(1)} %bitcast.7), custom_call_target="tpu_custom_call" | custom-call | tf_op jit(solution)/shard_map/pallas_call | solution.py:449
Async XLA Ops:
  0.6 19.0 %copy-start = (bf16[1024]{0:T(1024)(128)(2,1)S(1)}, bf16[1024]{0:T(1024)(128)(2,1)}, u32[]{:S(2)}) copy-start(bf16[1024]{0:T(1024)(128)(2,1)} %param.27) | copy-start | bytes 6148

commit v3 on v2

--- a/solution.py
+++ b/solution.py
@@ -13,10 +13,11 @@
 SIDES = 4
 SIDE = 4
 CHUNK = SIDES * SIDE
-PLAN = ((0,0,None,None),(1,1,0,None),(2,2,1,0),(3,3,None,None),(None,None,3,1),(None,None,2,3),(None,None,None,2))
+PLAN = ((((0, 0), (0, 1)), ((0, 0), (0, 1)), None, None),(((1, 0), (1, 1)), ((1, 0), (1, 1)), None, None),(((2, 0), (2, 1)), ((2, 0), (2, 1)), None, None),(((3, 1),), ((3, 1),), None, None),(((3, 0),), ((3, 0),), None, None),((), (), 1, None),((), (), 0, 1),((), (), None, 0))
 MESH = pl.DeviceIdType.MESH
 F32 = jnp.float32
 BF16 = jnp.bfloat16
+F8 = jnp.float8_e4m3fn
 
 
 def dense(values, weight):
@@ -151,16 +152,18 @@
         peer = me ^ jnp.where(k < n // 2, n // 2 + k, k + 1 - n // 2)
         pltpu.make_async_remote_copy(
             src_ref=send_ids.at[peer // n_row // span],
-            dst_ref=recv_ids.at[me],
+            dst_ref=recv_ids.at[my_row, my_table],
             send_sem=id_send,
-            recv_sem=id_recv.at[my_table // n_side],
+            recv_sem=id_recv.at[my_table // n_side, my_row],
             device_id=place(peer),
             device_id_type=MESH,
         ).start()
         return 0
 
     lax.fori_loop(0, n - 1, send_one, 0, unroll=4)
-    pltpu.make_async_copy(send_ids.at[own], recv_ids.at[me], id_recv.at[my_table // n_side]).start()
+    pltpu.make_async_copy(
+        send_ids.at[own], recv_ids.at[my_row, my_table], id_recv.at[my_table // n_side, my_row]
+    ).start()
 
     for load in loads[4:6]:
         load.wait()
@@ -180,13 +183,13 @@
     assert high_rows <= 256
     for r in range(0, rows, PROJECT):
         at = pl.ds(r, PROJECT)
-        flat_wide[at, :] = jnp.dot(
-            wt[at, :], wp[...], preferred_element_type=F32
+        flat_wide[:, at] = lax.dot_general(
+            wp[...], wt[at, :], (((0,), (1,)), ((), ())), preferred_element_type=F32
         ).astype(BF16)
         narrow = lax.dot_general(
-            nt[:, at], npj[...], (((0,), (0,)), ((), ())), preferred_element_type=F32
+            npj[...], nt[:, at], (((0,), (0,)), ((), ())), preferred_element_type=F32
         )
-        flat_narrow[at, :] = (narrow * (-1.0 / BASE)).astype(BF16)
+        flat_narrow[:, at] = (narrow * (-1.0 / BASE)).astype(BF16)
 
     at_high = lax.broadcasted_iota(jnp.int32, (high_rows, lanes), 0).astype(F32).astype(BF16)
     at_low = lax.broadcasted_iota(jnp.int32, (LOW, lanes), 0).astype(F32).astype(BF16)
@@ -209,47 +212,57 @@
         else:
             pl.loop(0, n_cc)(body)
 
-    def count(step, cc):
+    def taken(row, table):
+        ids = recv_ids[row, table] - first_row
+        high, low = [], []
+        for kind in range(2):
+            local = ids[kind : kind + 1, :]
+            key = (local >> (LOW.bit_length() - 1)) * batch + sample
+            key = jnp.where((key >= 0) & (key < high_rows), key, -1)
+            key = key.astype(F32).astype(BF16)
+            digit = (local & (LOW - 1)).astype(F32).astype(BF16)
+            high.append(jnp.where(key == at_high, marks[kind], zero))
+            low.append(jnp.where(digit == at_low, one, zero))
+        both = lax.dot_general(
+            jnp.concatenate(high, axis=1),
+            jnp.concatenate(low, axis=1),
+            (((1,), (1,)), ((), ())),
+            preferred_element_type=F32,
+        ).astype(BF16)
+        second = (both + shift) - shift
+        return both - second, second
+
+    def count(step, row, cc):
         first_k = side_of(step) * SIDE
-        for place_row in range(n_row):
-            row = lax.rem(my_row + place_row, n_row)
-            for k in range(SIDE):
-                at = (place_row * SIDE + k) * batch
-                ids = recv_ids[(first_k + k) * n_chunk + cc * n_row + row] - first_row
-                high, low = [], []
-                for kind in range(2):
-                    local = ids[kind : kind + 1, :]
-                    key = (local >> (LOW.bit_length() - 1)) * batch + sample
-                    key = jnp.where((key >= 0) & (key < high_rows), key, -1)
-                    key = key.astype(F32).astype(BF16)
-                    digit = (local & (LOW - 1)).astype(F32).astype(BF16)
-                    high.append(jnp.where(key == at_high, marks[kind], zero))
-                    low.append(jnp.where(digit == at_low, one, zero))
-                found = lax.dot_general(
-                    jnp.concatenate(high, axis=1),
-                    jnp.concatenate(low, axis=1),
+        mine = jnp.where(row == my_row, 0, 1)
+        for k in range(0, SIDE, 2):
+            table = (first_k + k) * n_cc + cc
+            at = pl.multiple_of(mine * 2 * SIDE * batch, 2 * SIDE * batch)
+            at = pl.ds(at + ((step % 2) * SIDE + k) * batch, 2 * batch)
+            found = zip(taken(row, table), taken(row, table + n_cc))
+            for kind, (here, there) in enumerate(found):
+                for h in range(high_count):
+                    own_rows = slice(h * batch, (h + 1) * batch)
+                    counts[step // 2, cc, kind, h, at, :] = jnp.concatenate(
+                        [here[own_rows], there[own_rows]], axis=0
+                    ).astype(F8)
+
+    def weigh(turn, cc):
+        given = 2 * SIDE * batch
+        for kind, flat in enumerate((flat_wide, flat_narrow)):
+            total = jnp.zeros((emb, n_row * given), F32)
+            for h in range(high_count):
+                total = total + lax.dot_general(
+                    flat[:, h * LOW : (h + 1) * LOW],
+                    counts[turn, cc, kind, h],
                     (((1,), (1,)), ((), ())),
                     preferred_element_type=F32,
-                ).astype(BF16)
-                for h in range(high_count):
-                    counts[step, cc, h, at : at + batch, :] = found[h * batch : (h + 1) * batch]
-
-    def weigh(step, cc):
-        wide = jnp.zeros((SIDE * n_row * batch, emb), F32)
-        narrow = jnp.zeros((SIDE * n_row * batch, emb), F32)
-        for h in range(high_count):
-            both = counts[step, cc, h]
-            second = (both + shift) - shift
-            first = both - second
-            at = slice(h * LOW, (h + 1) * LOW)
-            wide = wide + jnp.dot(first, flat_wide[at, :], preferred_element_type=F32)
-            narrow = narrow + jnp.dot(second, flat_narrow[at, :], preferred_element_type=F32)
-        given = SIDE * batch
-        for half, value in enumerate((wide, narrow)):
-            at = slice(half * emb, (half + 1) * emb)
-            give[step, cc, :, at] = value[:given].astype(BF16)
-            keep[step, cc, :, at] = value[given:]
-        pair_copy(step, cc).start()
+                )
+            total = total.T
+            at = slice(kind * emb, (kind + 1) * emb)
+            give[turn, cc, :, at] = total[:given].astype(BF16)
+            keep[turn, cc, :, at] = total[given:]
+        pair_copy(turn, cc).start()
 
     def pair_copy(step, cc):
         return pltpu.make_async_remote_copy(
@@ -261,38 +274,38 @@
             device_id_type=MESH,
         )
 
-    def arrive(step):
+    def arrive(step, row):
         side = side_of(step)
-        arrived = recv_ids.at[pl.ds(side * (n // SIDES), n // SIDES)]
-        pltpu.make_async_copy(arrived, arrived, id_recv.at[side]).wait()
-
-    def finish(step):
-        side = side_of(step)
-
+        arrived = recv_ids.at[row, pl.ds(side * n_side, n_side)]
+        pltpu.make_async_copy(arrived, arrived, id_recv.at[side, row]).wait()
+
+    def finish(turn):
         def block(cc):
-            pair_copy(step, cc).wait()
-            part[step, cc] = (keep[step, cc] + got[step, cc].astype(F32)).astype(BF16)
-            for k in range(SIDE):
-                peer = (side * SIDE + k) * n_cc + cc
-
-                pltpu.make_async_remote_copy(
-                    src_ref=part.at[step, cc, pl.ds(k * batch, batch)],
-                    dst_ref=recv_part.at[my_table],
-                    send_sem=part_send,
-                    recv_sem=part_recv,
-                    device_id=(peer, 1 - my_row),
-                    device_id_type=MESH,
-                ).start()
+            pair_copy(turn, cc).wait()
+            part[turn, cc] = (keep[turn, cc] + got[turn, cc].astype(F32)).astype(BF16)
+            for half in (1, 0):
+                side = side_of(2 * turn + half)
+                for k in range(SIDE):
+                    peer = (side * SIDE + k) * n_cc + cc
+                    at = (half * SIDE + k) * batch
+                    pltpu.make_async_remote_copy(
+                        src_ref=part.at[turn, cc, pl.ds(at, batch)],
+                        dst_ref=recv_part.at[my_table],
+                        send_sem=part_send,
+                        recv_sem=part_recv,
+                        device_id=(peer, 1 - my_row),
+                        device_id_type=MESH,
+                    ).start()
 
         each(block)
 
     for waits, counted, weighed, finished in PLAN:
-        if waits is not None:
-            arrive(waits)
+        for step, row in waits:
+            arrive(step, row)
 
         def block(cc):
-            if counted is not None:
-                count(counted, cc)
+            for step, row in counted:
+                count(step, row, cc)
             if weighed is not None:
                 weigh(weighed, cc)
 
@@ -341,9 +354,9 @@
     hidden = jnp.maximum(hidden, 0.0).astype(BF16)
     hid_ref[...] = hidden
 
-    pltpu.make_async_copy(
-        recv_ids.at[pl.ds(0, n - 1)], recv_ids.at[pl.ds(0, n - 1)], id_send
-    ).wait()
+    for row in range(n_row):
+        left = recv_ids.at[row, pl.ds(0, n_table - (1 if row else 0))]
+        pltpu.make_async_copy(left, left, id_send).wait()
     pltpu.make_async_copy(recv_part, recv_part, part_send).wait()
 
 
@@ -413,20 +426,20 @@
             pltpu.VMEM(narrow_projection.shape[1:], BF16),
             like(top_first),
             pltpu.VMEM((tables, 2, batch * slots), jnp.int32),
-            pltpu.VMEM((n, 2, batch * slots), jnp.int32),
-            pltpu.VMEM((SIDES, n_cc, rows // LOW, SIDE * n_row * batch, LOW), BF16),
-            pltpu.VMEM((rows, emb), BF16),
-            pltpu.VMEM((rows, emb), BF16),
-            *[pltpu.VMEM((SIDES, n_cc, SIDE * batch, 2 * emb), d) for d in (BF16, BF16, F32, BF16)],
+            pltpu.VMEM((n_row, n_table, 2, batch * slots), jnp.int32),
+            pltpu.VMEM((2, n_cc, 2, rows // LOW, 2 * SIDE * n_row * batch, LOW), F8),
+            pltpu.VMEM((emb, rows), BF16),
+            pltpu.VMEM((emb, rows), BF16),
+            *[pltpu.VMEM((2, n_cc, 2 * SIDE * batch, 2 * emb), d) for d in (BF16, BF16, F32, BF16)],
             pltpu.VMEM((n_table, batch, 2 * emb), BF16),
             pltpu.VMEM((1 + 2 * tables, batch, emb), F32),
             pltpu.SemaphoreType.DMA((13,)),
             pltpu.SemaphoreType.DMA,
-            pltpu.SemaphoreType.DMA((SIDES,)),
+            pltpu.SemaphoreType.DMA((SIDES, n_row)),
             pltpu.SemaphoreType.DMA,
             pltpu.SemaphoreType.DMA,
-            pltpu.SemaphoreType.DMA((SIDES, n_cc)),
-            pltpu.SemaphoreType.DMA((SIDES, n_cc)),
+            pltpu.SemaphoreType.DMA((2, n_cc)),
+            pltpu.SemaphoreType.DMA((2, n_cc)),
         ],
         compiler_params=pltpu.CompilerParams(
             collective_id=0, has_side_effects=True, vmem_limit_bytes=int(60 * 2**20)

time: 20.5 us -> 19.9 us (0.971)
  Pallas kernels: 19.6 us -> 19.1 us
    pallas_call x1, Pallas kernels: 18.9 us -> 18.4 us  [body(): pl.pallas_call(functools.partial(kernel, dims), out_shape=pltpu.VMEM((bat...]
where the time goes in v3:
time: 19.9 us; the launch traced here: 19.7 us
  Pallas kernels  19.1 us (96%)
  between operations  0.66 us (3%)
    pallas_call x1, Pallas kernels, body(): pl.pallas_call(functools.partial(kernel, dims), out_shape=pltpu.VMEM((bat...  18.4 us
    pallas_call x1, Pallas kernels, body(): pl.pallas_call(last_kernel, out_shape=(jax.ShapeDtypeStruct((batch, top),...  0.66 us

profile of v3, /device:TPU:0, one launch (start us, length us, event | category | flops | bytes accessed | tf_op | source)
XLA Modules:
  0.0 19.7 jit_solution(4132714181138152455)
XLA Ops:
  0.6 0.0 copy-start
  0.6 18.4 %shard_map.149.hid_ref = bf16[16,1024]{1,0:T(8,128)(2,1)S(1)} custom-call(bf16[16,13]{1,0:T(8,128)(2,1)} %x_hbm.1, bf16[13,512]{1,0:T(8,128)(2,1)} %bf_hbm.1, bf16[512,256]{1,0:T(8,128)(2,1)} %bs_hbm.1, bf16[256,128]{1,0:T(8,128)(2,1)} %bt_hbm.1, bf16[4096,256]{1,0:T(8,128)(2,1)} %wt_hbm.1, bf16[64,4096]{1,0:T(8,128)(2,1)} %bitcast.8, s32[4,8,16]{2,1,0:T(8,128)} %bitcast.9, ...), custom_call_target="tpu_custom_call" | custom-call | tf_op jit(solution)/shard_map/pallas_call | solution.py:409
  19.1 0.0 copy-done
  19.1 0.7 %shard_map.150 = (bf16[16,1024]{1,0:T(8,128)(2,1)}, f32[1,16]{1,0:T(1,128)}) custom-call(bf16[16,1024]{1,0:T(8,128)(2,1)S(1)} %shard_map.149.hid_ref, bf16[8,128]{1,0:T(8,128)(2,1)S(1)} %bitcast.7), custom_call_target="tpu_custom_call" | custom-call | tf_op jit(solution)/shard_map/pallas_call | solution.py:462
Async XLA Ops:
  0.6 18.4 %copy-start = (bf16[1024]{0:T(1024)(128)(2,1)S(1)}, bf16[1024]{0:T(1024)(128)(2,1)}, u32[]{:S(2)}) copy-start(bf16[1024]{0:T(1024)(128)(2,1)} %param.27) | copy-start | bytes 6148

commit v4 on v3

--- a/solution.py
+++ b/solution.py
@@ -8,12 +8,12 @@
 from jax.sharding import PartitionSpec as P
 
 LOW = 256
-PROJECT = 512
+PROJECT = 1024
 BASE = 32
 SIDES = 4
 SIDE = 4
 CHUNK = SIDES * SIDE
-PLAN = ((((0, 0), (0, 1)), ((0, 0), (0, 1)), None, None),(((1, 0), (1, 1)), ((1, 0), (1, 1)), None, None),(((2, 0), (2, 1)), ((2, 0), (2, 1)), None, None),(((3, 1),), ((3, 1),), None, None),(((3, 0),), ((3, 0),), None, None),((), (), 1, None),((), (), 0, 1),((), (), None, 0))
+PLAN = ((((0, 0), (0, 1)), ((0, 0), (0, 1)), (), ()), (((2, 0), (2, 1)), ((2, 0), (2, 1)), (), ()), (((3, 1),), ((3, 1),), (), ()), (((3, 0),), ((3, 0),), (), ()), ((), (), (1,), ()), (((1, 0), (1, 1)), ((1, 0), (1, 1)), (), ()), ((), (), (), (1,)), ((), (), (0,), ()), ((), (), (), (0,)))
 MESH = pl.DeviceIdType.MESH
 F32 = jnp.float32
 BF16 = jnp.bfloat16
@@ -181,15 +181,17 @@
     high_count = rows // LOW
     high_rows = high_count * batch
     assert high_rows <= 256
-    for r in range(0, rows, PROJECT):
-        at = pl.ds(r, PROJECT)
+    scaled = (npj[...].astype(F32) * (-1.0 / BASE)).astype(BF16)
+
+    @pl.loop(0, rows // PROJECT)
+    def _(r):
+        at = pl.ds(pl.multiple_of(r * PROJECT, PROJECT), PROJECT)
         flat_wide[:, at] = lax.dot_general(
             wp[...], wt[at, :], (((0,), (1,)), ((), ())), preferred_element_type=F32
         ).astype(BF16)
-        narrow = lax.dot_general(
-            npj[...], nt[:, at], (((0,), (0,)), ((), ())), preferred_element_type=F32
-        )
-        flat_narrow[:, at] = (narrow * (-1.0 / BASE)).astype(BF16)
+        flat_narrow[:, at] = lax.dot_general(
+            scaled, nt[:, at], (((0,), (0,)), ((), ())), preferred_element_type=F32
+        ).astype(BF16)
 
     at_high = lax.broadcasted_iota(jnp.int32, (high_rows, lanes), 0).astype(F32).astype(BF16)
     at_low = lax.broadcasted_iota(jnp.int32, (LOW, lanes), 0).astype(F32).astype(BF16)
@@ -201,10 +203,12 @@
     my_side = my_table // n_side
 
     def side_of(step):
-        if not step:
-            return my_side
-        side = SIDES - step
-        return jnp.where(side > my_side, side, side - 1)
+        side = SIDES - step if step in (0, 3) else 1 + step
+        if step:
+            side = jnp.where(side > my_side, side, side - 1)
+        else:
+            side = my_side
+        return jnp.where(my_side == 0, SIDES - 1 - step, side)
 
     def each(body):
         if n_cc == 1:
@@ -258,10 +262,8 @@
                     (((1,), (1,)), ((), ())),
                     preferred_element_type=F32,
                 )
-            total = total.T
-            at = slice(kind * emb, (kind + 1) * emb)
-            give[turn, cc, :, at] = total[:given].astype(BF16)
-            keep[turn, cc, :, at] = total[given:]
+            give[turn, cc, kind] = total[:, :given].astype(BF16)
+            keep[turn, cc, kind] = total[:, given:]
         pair_copy(turn, cc).start()
 
     def pair_copy(step, cc):
@@ -282,7 +284,9 @@
     def finish(turn):
         def block(cc):
             pair_copy(turn, cc).wait()
-            part[turn, cc] = (keep[turn, cc] + got[turn, cc].astype(F32)).astype(BF16)
+            for kind in range(2):
+                total = keep[turn, cc, kind] + got[turn, cc, kind].astype(F32)
+                part[turn, cc, :, kind * emb : (kind + 1) * emb] = total.astype(BF16).T
             for half in (1, 0):
                 side = side_of(2 * turn + half)
                 for k in range(SIDE):
@@ -306,12 +310,12 @@
         def block(cc):
             for step, row in counted:
                 count(step, row, cc)
-            if weighed is not None:
-                weigh(weighed, cc)
+            for turn in weighed:
+                weigh(turn, cc)
 
         each(block)
-        if finished is not None:
-            finish(finished)
+        for turn in finished:
+            finish(turn)
 
     pltpu.make_async_copy(recv_part, recv_part, part_recv).wait()
 
@@ -430,7 +434,8 @@
             pltpu.VMEM((2, n_cc, 2, rows // LOW, 2 * SIDE * n_row * batch, LOW), F8),
             pltpu.VMEM((emb, rows), BF16),
             pltpu.VMEM((emb, rows), BF16),
-            *[pltpu.VMEM((2, n_cc, 2 * SIDE * batch, 2 * emb), d) for d in (BF16, BF16, F32, BF16)],
+            *[pltpu.VMEM((2, n_cc, 2, emb, 2 * SIDE * batch), d) for d in (BF16, BF16, F32)],
+            pltpu.VMEM((2, n_cc, 2 * SIDE * batch, 2 * emb), BF16),
             pltpu.VMEM((n_table, batch, 2 * emb), BF16),
             pltpu.VMEM((1 + 2 * tables, batch, emb), F32),
             pltpu.SemaphoreType.DMA((13,)),

time: 19.9 us -> 19.7 us (0.990)
  Pallas kernels: 19.1 us -> 18.9 us
where the time goes in v4:
time: 19.7 us; the launch traced here: 19.5 us
  Pallas kernels  18.9 us (96%)
  between operations  0.66 us (3%)
    pallas_call x1, Pallas kernels, body(): pl.pallas_call(functools.partial(kernel, dims), out_shape=pltpu.VMEM((bat...  18.2 us
    pallas_call x1, Pallas kernels, body(): pl.pallas_call(last_kernel, out_shape=(jax.ShapeDtypeStruct((batch, top),...  0.66 us

profile of v4, /device:TPU:0, one launch (start us, length us, event | category | flops | bytes accessed | tf_op | source)
XLA Modules:
  0.0 19.5 jit_solution(6907457046221395832)
XLA Ops:
  0.6 0.0 copy-start
  0.6 18.2 %shard_map.149.hid_ref = bf16[16,1024]{1,0:T(8,128)(2,1)S(1)} custom-call(bf16[16,13]{1,0:T(8,128)(2,1)} %x_hbm.1, bf16[13,512]{1,0:T(8,128)(2,1)} %bf_hbm.1, bf16[512,256]{1,0:T(8,128)(2,1)} %bs_hbm.1, bf16[256,128]{1,0:T(8,128)(2,1)} %bt_hbm.1, bf16[4096,256]{1,0:T(8,128)(2,1)} %wt_hbm.1, bf16[64,4096]{1,0:T(8,128)(2,1)} %bitcast.8, s32[4,8,16]{2,1,0:T(8,128)} %bitcast.9, ...), custom_call_target="tpu_custom_call" | custom-call | tf_op jit(solution)/shard_map/pallas_call | solution.py:413
  18.9 0.0 copy-done
  18.9 0.7 %shard_map.150 = (bf16[16,1024]{1,0:T(8,128)(2,1)}, f32[1,16]{1,0:T(1,128)}) custom-call(bf16[16,1024]{1,0:T(8,128)(2,1)S(1)} %shard_map.149.hid_ref, bf16[8,128]{1,0:T(8,128)(2,1)S(1)} %bitcast.7), custom_call_target="tpu_custom_call" | custom-call | tf_op jit(solution)/shard_map/pallas_call | solution.py:467
Async XLA Ops:
  0.6 18.2 %copy-start = (bf16[1024]{0:T(1024)(128)(2,1)S(1)}, bf16[1024]{0:T(1024)(128)(2,1)}, u32[]{:S(2)}) copy-start(bf16[1024]{0:T(1024)(128)(2,1)} %param.27) | copy-start | bytes 6148

commit v5 on v4

--- a/solution.py
+++ b/solution.py
@@ -149,7 +149,7 @@
     pl.semaphore_wait(barrier, n - 1)
 
     def send_one(k, _):
-        peer = me ^ jnp.where(k < n // 2, n // 2 + k, k + 1 - n // 2)
+        peer = me ^ (n - 1 - k)
         pltpu.make_async_remote_copy(
             src_ref=send_ids.at[peer // n_row // span],
             dst_ref=recv_ids.at[my_row, my_table],

time: 19.7 us -> 19.6 us (level)
  Pallas kernels: 18.9 us -> 18.7 us
where the time goes in v5:
time: 19.6 us; the launch traced here: 19.4 us
  Pallas kernels  18.7 us (95%)
  between operations  0.66 us (3%)
    pallas_call x1, Pallas kernels, body(): pl.pallas_call(functools.partial(kernel, dims), out_shape=pltpu.VMEM((bat...  18.1 us
    pallas_call x1, Pallas kernels, body(): pl.pallas_call(last_kernel, out_shape=(jax.ShapeDtypeStruct((batch, top),...  0.66 us

profile of v5, /device:TPU:0, one launch (start us, length us, event | category | flops | bytes accessed | tf_op | source)
XLA Modules:
  0.0 19.4 jit_solution(1372701748583854184)
XLA Ops:
  0.6 0.0 copy-start
  0.6 18.1 %shard_map.149.hid_ref = bf16[16,1024]{1,0:T(8,128)(2,1)S(1)} custom-call(bf16[16,13]{1,0:T(8,128)(2,1)} %x_hbm.1, bf16[13,512]{1,0:T(8,128)(2,1)} %bf_hbm.1, bf16[512,256]{1,0:T(8,128)(2,1)} %bs_hbm.1, bf16[256,128]{1,0:T(8,128)(2,1)} %bt_hbm.1, bf16[4096,256]{1,0:T(8,128)(2,1)} %wt_hbm.1, bf16[64,4096]{1,0:T(8,128)(2,1)} %bitcast.8, s32[4,8,16]{2,1,0:T(8,128)} %bitcast.9, ...), custom_call_target="tpu_custom_call" | custom-call | tf_op jit(solution)/shard_map/pallas_call | solution.py:413
  18.7 0.0 copy-done
  18.7 0.7 %shard_map.150 = (bf16[16,1024]{1,0:T(8,128)(2,1)}, f32[1,16]{1,0:T(1,128)}) custom-call(bf16[16,1024]{1,0:T(8,128)(2,1)S(1)} %shard_map.149.hid_ref, bf16[8,128]{1,0:T(8,128)(2,1)S(1)} %bitcast.7), custom_call_target="tpu_custom_call" | custom-call | tf_op jit(solution)/shard_map/pallas_call | solution.py:467
Async XLA Ops:
  0.6 18.1 %copy-start = (bf16[1024]{0:T(1024)(128)(2,1)S(1)}, bf16[1024]{0:T(1024)(128)(2,1)}, u32[]{:S(2)}) copy-start(bf16[1024]{0:T(1024)(128)(2,1)} %param.27) | copy-start | bytes 6148
